TPU v7x, 32 devices: a whole 2x2x4 slice. The times are simulated.
32 devices in a mesh: row: 8 (over z, x), col: 4 (over y, core).
Axes of the slice: x: 2, y: 2, z: 4, core: 2. Of those that a mesh axis runs over, the one named last changes fastest.
Arguments:
- snapshot: bfloat16 [512, 256, 512], P('row', 'col'), may hold values from -6 to 6
- basis_two: bfloat16 [256, 128], P('col'), may hold values from -0.375 to 0.375
- basis_three: bfloat16 [512, 128], replicated, may hold values from -0.25 to 0.25
Outputs:
- gram: float32 [512, 512], P('row', 'col')
All inputs are finite; a program needn't handle non-finite values.
Results may differ from a plain program's by a relative error of at most 0.0017.
Values may be sent and summed in bfloat16 or wider, within the bound.
No kernel may reach another device: no remote copies, remote signals or barrier semaphores. Data moves between devices by JAX's collectives and lax.ppermute only.
A program may use at most 64 MiB of HBM per device.

v0:
```python
import jax
import jax.numpy as jnp
from jax import lax
from jax.sharding import PartitionSpec as P


def on_device(snapshot, basis_two, basis_three):
    cells_one, cells_two, cells_three = snapshot.shape
    ranks_two = basis_two.shape[1]
    ranks_three = basis_three.shape[1]
    inner = jnp.dot(
        snapshot.reshape(cells_one * cells_two, cells_three),
        basis_three,
        preferred_element_type=jnp.float32,
    )
    inner = inner.astype(jnp.bfloat16).reshape(cells_one, cells_two, ranks_three)
    regrouped = lax.all_to_all(inner, "col", split_axis=2, concat_axis=1, tiled=True)
    whole_factor = lax.all_gather(basis_two, "col", axis=0, tiled=True)
    full = jnp.einsum("abr,bq->qar", regrouped, whole_factor, preferred_element_type=jnp.float32)
    rounded = lax.all_to_all(
        full.astype(jnp.bfloat16), "col", split_axis=0, concat_axis=2, tiled=True
    )
    partial_gram = jnp.einsum(
        "qar,qbr->ab",
        rounded,
        lax.all_gather(rounded, "row", axis=1, tiled=True),
        preferred_element_type=jnp.float32,
    )
    summed_gram = lax.psum_scatter(partial_gram, "col", scatter_dimension=1, tiled=True)
    return summed_gram * (1.0 / (ranks_two * ranks_three))


def solution(mesh):
    in_specs = (P("row", "col", None), P("col", None), P())
    out_specs = P("row", "col")
    return jax.shard_map(
        on_device, mesh=mesh, in_specs=in_specs, out_specs=out_specs, check_vma=False
    )
```

profile of v0, /device:TPU:0, one launch (start us, length us, event | category | flops | bytes accessed | tf_op | source)
XLA Modules:
  0.0 165.3 jit_solution(16451007527104671222)
XLA Ops:
  6.5 0.0 copy-start
  6.5 0.9 copy-done
  7.4 3.4 %convolution_convert_fusion = bf16[4096,128]{1,0:T(8,128)(2,1)S(1)} fusion(bf16[4096,512]{1,0:T(8,128)(2,1)} %bitcast.31, bf16[512,128]{1,0:T(8,128)(2,1)S(1)} %copy-done), kind=kOutput, calls=%fused_computation | convolution fusion | flops 537395200 | bytes 5373952 | tf_op jit(solution)/shard_map/dot_general | solution.py:11
  10.9 0.0 copy-start.1
  10.9 3.0 %copy.20 = bf16[64,64,128]{1,0,2:T(8,128)(2,1)S(1)} copy(bf16[64,64,128]{2,1,0:T(8,128)(2,1)S(1)} %bitcast.32) | data formatting | bytes 2097152 | tf_op jit(solution)/shard_map/reshape | solution.py:16
  13.9 2.6 %reshape.10 = bf16[4,2,65536]{2,1,0:T(2,128)(2,1)} reshape(bf16[128,64,64]{2,1,0:T(8,128)(2,1)S(1)} %bitcast.29) | data formatting | bytes 2097152
  16.5 4.3 %all-to-all-start = ((bf16[4,2,65536]{2,1,0:T(2,128)(2,1)}), bf16[4,2,65536]{2,1,0:T(2,128)(2,1)S(1)}, u32[]{:S(2)}, u32[]{:S(2)}) async-start(bf16[4,2,65536]{2,1,0:T(2,128)(2,1)} %reshape.10), calls=%async_computation | async-start | bytes 2097152 | tf_op jit(solution)/shard_map/all_to_all | solution.py:17
  20.8 0.0 all-gather.2.cloned.1.call-start
  20.8 0.0 copy-done.1
  20.8 15.6 %all_gather.6 = bf16[256,128]{1,0:T(8,128)(2,1)S(1)} all-gather(bf16[64,128]{1,0:T(8,128)(2,1)S(1)} %copy-done.1), channel_id=1, replica_groups=mesh['row'=8,'col'=4] {'col'}, dimensions={0}, use_global_device_ids=true | all-gather | bytes 81920 | tf_op jit(solution)/shard_map/all_gather | solution.py:18
  36.4 0.0 all-to-all-done
  36.4 1.4 reshape.11
  37.8 3.0 %copy.22 = bf16[64,4,64,32]{2,1,3,0:T(4,128)(2,1)} copy(bf16[64,4,64,32]{2,0,3,1:T(8,128)(2,1)S(1)} %bitcast.30) | data formatting | bytes 2097152 | tf_op jit(solution)/shard_map/all_to_all | solution.py:17
  40.8 3.5 %all_to_all.29 = bf16[64,256,32]{1,2,0:T(8,128)(2,1)S(1)} reshape(bf16[64,4,64,32]{2,1,3,0:T(4,128)(2,1)} %copy.22) | data formatting | bytes 2097152 | tf_op jit(solution)/shard_map/all_to_all | solution.py:17
  44.3 0.4 fusion
  44.7 1.7 %copy.23 = bf16[128,64,32]{1,2,0:T(8,128)(2,1)S(1)} copy(bf16[128,64,32]{0,2,1:T(8,128)(2,1)S(1)} %fusion) | data formatting | bytes 1048576 | tf_op jit(solution)/shard_map/convert_element_type | solution.py:21
  46.4 0.9 reshape.12
  47.3 11.2 %all_to_all.36 = bf16[4,2,32768]{2,1,0:T(2,128)(2,1)S(1)} all-to-all(bf16[4,2,32768]{2,1,0:T(2,128)(2,1)S(1)} %reshape.12), channel_id=1, replica_groups=mesh['row'=8,'col'=4] {'col'}, dimensions={0} | all-to-all | bytes 1048576 | tf_op jit(solution)/shard_map/all_to_all | solution.py:20
  58.5 0.7 reshape.13
  59.2 0.1 copy.24
  59.4 1.1 copy.25
  60.5 0.0 all-gather.2.cloned.1.call-update
  60.5 0.0 reduce-scatter.2.cloned.1.call-start
  60.6 73.9 %all-gather.2.cloned.1.call-done = bf16[32,512,128]{2,1,0:T(8,128)(2,1)} async-done(((bf16[32,64,128]{2,1,0:T(8,128)(2,1)}), bf16[32,512,128]{2,1,0:T(8,128)(2,1)}) %all-gather.2.cloned.1.call-update) | async-done | bytes 4194320 | tf_op jit(solution)/shard_map/all_gather | solution.py:26
  134.4 4.2 %convolution_bitcast_fusion = f32[64,512]{1,0:T(8,128)} fusion(bf16[32,64,128]{1,2,0:T(8,128)(2,1)S(1)} %bitcast.28, bf16[32,512,128]{2,1,0:T(8,128)(2,1)} %all-gather.2.cloned.1.call-done), kind=kOutput, calls=%fused_computation.3 | convolution fusion | flops 268435456 | bytes 4849664 | tf_op jit(solution)/shard_map/qar,qbr->ab/dot_general | solution.py:23
  138.7 0.0 reduce-scatter.2.cloned.1.call-update
  138.7 18.3 %reduce-scatter.2.cloned.1.call-done = f32[64,128]{1,0:T(8,128)} async-done(((f32[64,512]{1,0:T(8,128)}), f32[64,128]{1,0:T(8,128)}) %reduce-scatter.2.cloned.1.call-update) | async-done | bytes 32784 | tf_op jit(solution)/shard_map/reduce_scatter | solution.py:29
  157.0 1.4 broadcast_multiply_fusion
Async XLA Ops:
  6.5 0.9 copy-start
  10.9 9.9 %copy-start.1 = (bf16[64,128]{1,0:T(8,128)(2,1)S(1)}, bf16[64,128]{1,0:T(8,128)(2,1)}, u32[]{:S(2)}) copy-start(bf16[64,128]{1,0:T(8,128)(2,1)} %param.4) | copy-start | bytes 49156
  16.5 19.9 %all-to-all-start = ((bf16[4,2,65536]{2,1,0:T(2,128)(2,1)}), bf16[4,2,65536]{2,1,0:T(2,128)(2,1)S(1)}, u32[]{:S(2)}, u32[]{:S(2)}) async-start(bf16[4,2,65536]{2,1,0:T(2,128)(2,1)} %reshape.10), calls=%async_computation | async-start | bytes 2097152 | tf_op jit(solution)/shard_map/all_to_all | solution.py:17
  20.8 113.7 %all-gather.2.cloned.1.call-start = ((), (), s32[]{:S(2)}) async-start(), calls=%async_computation.3 | async-start | bytes 4718592 | tf_op jit(solution)/shard_map/all_gather | solution.py:26
  60.5 96.5 %reduce-scatter.2.cloned.1.call-start = ((), (), s32[]{:S(2)}) async-start(), calls=%async_computation.4 | async-start | bytes 163840 | tf_op jit(solution)/shard_map/reduce_scatter | solution.py:29
Sparse Core Ops, SparseCore 0:
  60.6 73.7 all-gather.1
  138.8 18.1 reduce-scatter.1
where the time goes:
time: 166 us; the launch traced here: 165 us
  waiting for transfers between devices  92.3 us (56%)
  blocking collectives  26.8 us (16%)
  local copies, waits for them, and re-layouts  18.9 us (11%)
  between operations  13.5 us (8%)
  matrix products  8.09 us (5%)
  starting transfers between devices  4.3 us (3%)
    all_gather x1, waiting for transfers between devices, on_device(): lax.all_gather(rounded, 'row', axis=1, tiled=True)  73.9 us
    reduce_scatter x1, waiting for transfers between devices, on_device(): lax.psum_scatter(partial_gram, 'col', scatter_dimension=1, tiled=True)  18.3 us
    all_gather x1, blocking collectives, on_device(): whole_factor = lax.all_gather(basis_two, 'col', axis=0, tiled=True)  15.6 us
    all_to_all x1, blocking collectives, on_device(): lax.all_to_all(full.astype(jnp.bfloat16), 'col', split_axis=0, concat_axi...  11.2 us
    unnamed x8, local copies, waits for them, and re-layouts  6.55 us
    all_to_all x2, local copies, waits for them, and re-layouts, on_device(): lax.all_to_all(inner, 'col', split_axis=2, concat_axis=1, tiled=True)  6.45 us
    all_to_all x1, starting transfers between devices, on_device(): lax.all_to_all(inner, 'col', split_axis=2, concat_axis=1, tiled=True)  4.26 us
    dot_general x1, matrix products, on_device(): jnp.einsum('qar,qbr->ab', rounded, lax.all_gather(rounded, 'row', axis=1,...  4.22 us
  transfers between devices with their start and end apart: 3, of which 2 were waited for; matrix products, arithmetic and copies ran while one was open for 0% of the time, Pallas kernels for 0%

commit v1 on v0

--- a/solution.py
+++ b/solution.py
@@ -15,8 +15,37 @@
     )
     inner = inner.astype(jnp.bfloat16).reshape(cells_one, cells_two, ranks_three)
     regrouped = lax.all_to_all(inner, "col", split_axis=2, concat_axis=1, tiled=True)
-    whole_factor = lax.all_gather(basis_two, "col", axis=0, tiled=True)
-    full = jnp.einsum("abr,bq->qar", regrouped, whole_factor, preferred_element_type=jnp.float32)
+    devices, position, extent = (lax.axis_size("col"), lax.axis_index("col"), basis_two.shape[0])
+    ahead = [(i, (i + 1) % devices) for i in range(devices)]
+    behind = [(i, (i - 1) % devices) for i in range(devices)]
+    middle = devices // 2
+    from_left = from_right = basis_two
+    full = jnp.einsum(
+        "abr,bq->qar",
+        lax.dynamic_slice_in_dim(regrouped, position * extent, basis_two.shape[0], axis=1),
+        basis_two,
+        preferred_element_type=jnp.float32,
+    )
+    for step in range(1, middle + 1):
+        from_left = lax.ppermute(from_left, "col", ahead)
+        if step < devices - middle:
+            from_right = lax.ppermute(from_right, "col", behind)
+            full = full + jnp.einsum(
+                "abr,bq->qar",
+                lax.dynamic_slice_in_dim(
+                    regrouped, (position + step) % devices * extent, from_right.shape[0], axis=1
+                ),
+                from_right,
+                preferred_element_type=jnp.float32,
+            )
+        full = full + jnp.einsum(
+            "abr,bq->qar",
+            lax.dynamic_slice_in_dim(
+                regrouped, (position - step) % devices * extent, from_left.shape[0], axis=1
+            ),
+            from_left,
+            preferred_element_type=jnp.float32,
+        )
     rounded = lax.all_to_all(
         full.astype(jnp.bfloat16), "col", split_axis=0, concat_axis=2, tiled=True
     )

time: 166 us -> 166 us (level)
  blocking collectives: 26.8 us -> 11.2 us
  waiting for transfers between devices: 92.3 us -> 105 us
  starting transfers between devices: 4.3 us -> 6.16 us
    all_gather x1 -> x0, blocking collectives: 15.6 us -> none  [on_device(): whole_factor = lax.all_gather(basis_two, 'col', axis=0, tiled=True)]
    ppermute x0 -> x3, waiting for transfers between devices: none -> 12.1 us  [the longest x2 12.1 us: on_device(): from_left = lax.ppermute(from_left, 'col', ahead)]
    ppermute x0 -> x3, starting transfers between devices: none -> 1.86 us  [the longest x1 1.35 us: on_device(): from_right = lax.ppermute(from_right, 'col', behind)]
  transfers between devices with their start and end apart: 3 -> 6, of which waited for: 2 -> 4; matrix products, arithmetic and copies ran while one was open for 0% -> 3% of each run, Pallas kernels for 0% -> 0%
where the time goes in v1:
time: 166 us; the launch traced here: 165 us
  waiting for transfers between devices  105 us (63%)
  local copies, waits for them, and re-layouts  18.9 us (11%)
  between operations  13.5 us (8%)
  blocking collectives  11.2 us (7%)
  matrix products  9.09 us (5%)
  starting transfers between devices  6.16 us (4%)
    all_gather x1, waiting for transfers between devices, on_device(): lax.all_gather(rounded, 'row', axis=1, tiled=True)  73.9 us
    reduce_scatter x1, waiting for transfers between devices, on_device(): lax.psum_scatter(partial_gram, 'col', scatter_dimension=1, tiled=True)  18.3 us
    ppermute x2, waiting for transfers between devices, on_device(): from_left = lax.ppermute(from_left, 'col', ahead)  12.1 us
    all_to_all x1, blocking collectives, on_device(): lax.all_to_all(full.astype(jnp.bfloat16), 'col', split_axis=0, concat_axi...  11.2 us
    unnamed x8, local copies, waits for them, and re-layouts  6.56 us
    all_to_all x2, local copies, waits for them, and re-layouts, on_device(): lax.all_to_all(inner, 'col', split_axis=2, concat_axis=1, tiled=True)  6.43 us
    all_to_all x1, starting transfers between devices, on_device(): lax.all_to_all(inner, 'col', split_axis=2, concat_axis=1, tiled=True)  4.26 us
    dot_general x1, matrix products, on_device(): jnp.einsum('qar,qbr->ab', rounded, lax.all_gather(rounded, 'row', axis=1,...  4.23 us
  transfers between devices with their start and end apart: 6, of which 4 were waited for; matrix products, arithmetic and copies ran while one was open for 3% of the time, Pallas kernels for 0%

profile of v1, /device:TPU:0, one launch (start us, length us, event | category | flops | bytes accessed | tf_op | source)
XLA Modules:
  0.0 165.3 jit_solution(3806480527712715819)
XLA Ops:
  6.5 0.0 copy-start
  6.5 0.9 copy-done
  7.4 3.4 %convolution_convert_fusion = bf16[4096,128]{1,0:T(8,128)(2,1)S(1)} fusion(bf16[4096,512]{1,0:T(8,128)(2,1)} %bitcast.39, bf16[512,128]{1,0:T(8,128)(2,1)S(1)} %copy-done), kind=kOutput, calls=%fused_computation | convolution fusion | flops 537395200 | bytes 5373952 | tf_op jit(solution)/shard_map/dot_general | solution.py:11
  10.9 0.0 copy-start.1
  10.9 3.0 %copy.20 = bf16[64,64,128]{1,0,2:T(8,128)(2,1)S(1)} copy(bf16[64,64,128]{2,1,0:T(8,128)(2,1)S(1)} %bitcast.40) | data formatting | bytes 2097152 | tf_op jit(solution)/shard_map/reshape | solution.py:16
  13.9 2.7 %reshape.13 = bf16[4,2,65536]{2,1,0:T(2,128)(2,1)} reshape(bf16[128,64,64]{2,1,0:T(8,128)(2,1)S(1)} %bitcast.37) | data formatting | bytes 2097152
  16.5 4.3 %all-to-all-start = ((bf16[4,2,65536]{2,1,0:T(2,128)(2,1)}), bf16[4,2,65536]{2,1,0:T(2,128)(2,1)S(1)}, u32[]{:S(2)}, u32[]{:S(2)}) async-start(bf16[4,2,65536]{2,1,0:T(2,128)(2,1)} %reshape.13), calls=%async_computation | async-start | bytes 2097152 | tf_op jit(solution)/shard_map/all_to_all | solution.py:17
  20.8 0.0 all-gather.2.cloned.1.call-start
  20.8 0.0 copy-done.1
  20.8 0.5 collective-permute-start.1
  21.3 1.4 collective-permute-start
  22.7 12.1 %collective-permute-done.1 = bf16[64,128]{1,0:T(8,128)(2,1)S(1)} collective-permute-done((bf16[64,128]{1,0:T(8,128)(2,1)S(1)}, bf16[64,128]{1,0:T(8,128)(2,1)S(1)}, u32[]{:S(2)}, u32[]{:S(2)}) %collective-permute-start.1) | collective-permute-done | bytes 16416 | tf_op jit(solution)/shard_map/ppermute | solution.py:30
  34.8 0.0 collective-permute-start.2
  34.8 0.6 all-to-all-done
  35.4 1.4 reshape.14
  36.8 3.0 %copy.22 = bf16[64,4,64,32]{2,1,3,0:T(4,128)(2,1)} copy(bf16[64,4,64,32]{2,0,3,1:T(8,128)(2,1)S(1)} %bitcast.38) | data formatting | bytes 2097152 | tf_op jit(solution)/shard_map/all_to_all | solution.py:17
  39.8 3.5 %all_to_all.29 = bf16[64,256,32]{1,2,0:T(8,128)(2,1)S(1)} reshape(bf16[64,4,64,32]{2,1,3,0:T(4,128)(2,1)} %copy.22) | data formatting | bytes 2097152 | tf_op jit(solution)/shard_map/all_to_all | solution.py:17
  43.3 0.4 fusion.5
  43.6 0.0 collective-permute-done
  43.7 0.4 convolution_add_fusion.2
  44.0 0.4 convolution_add_fusion.1
  44.4 0.0 collective-permute-done.2
  44.4 0.4 fusion.1
  44.8 1.7 %copy.23 = bf16[128,64,32]{1,2,0:T(8,128)(2,1)S(1)} copy(bf16[128,64,32]{0,2,1:T(8,128)(2,1)S(1)} %fusion.1) | data formatting | bytes 1048576 | tf_op jit(solution)/shard_map/convert_element_type | solution.py:50
  46.5 0.9 reshape.15
  47.3 11.2 %all_to_all.36 = bf16[4,2,32768]{2,1,0:T(2,128)(2,1)S(1)} all-to-all(bf16[4,2,32768]{2,1,0:T(2,128)(2,1)S(1)} %reshape.15), channel_id=1, replica_groups=mesh['row'=8,'col'=4] {'col'}, dimensions={0} | all-to-all | bytes 1048576 | tf_op jit(solution)/shard_map/all_to_all | solution.py:49
  58.5 0.7 reshape.16
  59.3 0.1 copy.24
  59.4 1.1 copy.25
  60.5 0.0 all-gather.2.cloned.1.call-update
  60.6 0.0 reduce-scatter.2.cloned.1.call-start
  60.6 73.9 %all-gather.2.cloned.1.call-done = bf16[32,512,128]{2,1,0:T(8,128)(2,1)} async-done(((bf16[32,64,128]{2,1,0:T(8,128)(2,1)}), bf16[32,512,128]{2,1,0:T(8,128)(2,1)}) %all-gather.2.cloned.1.call-update) | async-done | bytes 4194320 | tf_op jit(solution)/shard_map/all_gather | solution.py:55
  134.5 4.2 %convolution_bitcast_fusion = f32[64,512]{1,0:T(8,128)} fusion(bf16[32,64,128]{1,2,0:T(8,128)(2,1)S(1)} %bitcast.36, bf16[32,512,128]{2,1,0:T(8,128)(2,1)} %all-gather.2.cloned.1.call-done), kind=kOutput, calls=%fused_computation.6 | convolution fusion | flops 268435456 | bytes 4849664 | tf_op jit(solution)/shard_map/qar,qbr->ab/dot_general | solution.py:52
  138.7 0.0 reduce-scatter.2.cloned.1.call-update
  138.8 18.3 %reduce-scatter.2.cloned.1.call-done = f32[64,128]{1,0:T(8,128)} async-done(((f32[64,512]{1,0:T(8,128)}), f32[64,128]{1,0:T(8,128)}) %reduce-scatter.2.cloned.1.call-update) | async-done | bytes 32784 | tf_op jit(solution)/shard_map/reduce_scatter | solution.py:58
  157.1 1.4 broadcast_multiply_fusion
Async XLA Ops:
  6.5 0.9 copy-start
  10.9 9.9 %copy-start.1 = (bf16[64,128]{1,0:T(8,128)(2,1)S(1)}, bf16[64,128]{1,0:T(8,128)(2,1)}, u32[]{:S(2)}) copy-start(bf16[64,128]{1,0:T(8,128)(2,1)} %param.4) | copy-start | bytes 49156
  16.5 18.9 %all-to-all-start = ((bf16[4,2,65536]{2,1,0:T(2,128)(2,1)}), bf16[4,2,65536]{2,1,0:T(2,128)(2,1)S(1)}, u32[]{:S(2)}, u32[]{:S(2)}) async-start(bf16[4,2,65536]{2,1,0:T(2,128)(2,1)} %reshape.13), calls=%async_computation | async-start | bytes 2097152 | tf_op jit(solution)/shard_map/all_to_all | solution.py:17
  20.8 113.7 %all-gather.2.cloned.1.call-start = ((), (), s32[]{:S(2)}) async-start(), calls=%async_computation.3 | async-start | bytes 4718592 | tf_op jit(solution)/shard_map/all_gather | solution.py:55
  20.8 14.0 %collective-permute-start.1 = (bf16[64,128]{1,0:T(8,128)(2,1)S(1)}, bf16[64,128]{1,0:T(8,128)(2,1)S(1)}, u32[]{:S(2)}, u32[]{:S(2)}) collective-permute-start(bf16[64,128]{1,0:T(8,128)(2,1)S(1)} %copy-done.1), channel_id=1, source_target_pairs={{0,1},{1,2},{2,3},{3,0},{4,5},{5,6},{6,7},{7,4},{8,9},{9,10},{10,1... | collective-permute-start | bytes 49160 | tf_op jit(solution)/shard_map/ppermute | solution.py:30
  21.3 22.3 %collective-permute-start = (bf16[64,128]{1,0:T(8,128)(2,1)S(1)}, bf16[64,128]{1,0:T(8,128)(2,1)S(1)}, u32[]{:S(2)}, u32[]{:S(2)}) collective-permute-start(bf16[64,128]{1,0:T(8,128)(2,1)S(1)} %copy-done.1), channel_id=1, source_target_pairs={{0,3},{1,0},{2,1},{3,2},{4,7},{5,4},{6,5},{7,6},{8,11},{9,8},{10,9... | collective-permute-start | bytes 49160 | tf_op jit(solution)/shard_map/ppermute | solution.py:32
  34.8 9.6 %collective-permute-start.2 = (bf16[64,128]{1,0:T(8,128)(2,1)S(1)}, bf16[64,128]{1,0:T(8,128)(2,1)S(1)}, u32[]{:S(2)}, u32[]{:S(2)}) collective-permute-start(bf16[64,128]{1,0:T(8,128)(2,1)S(1)} %collective-permute-done.1), channel_id=1, source_target_pairs={{0,1},{1,2},{2,3},{3,0},{4,5},{5,6},{6,7},{7,4},{8,9},{9,10},{10,1... | collective-permute-start | bytes 49160 | tf_op jit(solution)/shard_map/ppermute | solution.py:30
  60.6 96.5 %reduce-scatter.2.cloned.1.call-start = ((), (), s32[]{:S(2)}) async-start(), calls=%async_computation.4 | async-start | bytes 163840 | tf_op jit(solution)/shard_map/reduce_scatter | solution.py:58
Sparse Core Ops, SparseCore 0:
  60.7 73.7 all-gather.1
  138.9 18.1 reduce-scatter.1
